TPU v7x, 32 devices: a whole 2x2x4 slice. The times are simulated.
32 devices in a mesh: rows: 8 (over z, x), cols: 4 (over y, core).
Axes of the slice: x: 2, y: 2, z: 4, core: 2. Of those that a mesh axis runs over, the one named last changes fastest.
Arguments:
- tables: float32 [4, 4096, 512], P(None, 'rows', 'cols'), may hold values from -1.5 to 1.5
- dense_features: float32 [256, 512], P('rows', 'cols'), may hold values from -6 to 6
- slot_rows: int32 [8, 8, 4, 64], P('rows'), may hold values from 0 to 511, as said below
- slot_examples: int32 [8, 8, 4, 64], P('rows'), may hold values from 0 to 31, as said below
- slot_counts: int32 [8, 8, 4], P('rows'), may hold values from 21 to 64, as said below
Outputs:
- pooled: float32 [256, 4, 512], P('rows', None, 'cols')
- interactions: float32 [256, 10], P('rows')
Inputs may be any that keep to these rules, and one draw needn't show every extreme that they name: slot_rows[s, o, t, c] names row o * 512 + value of table t. `slot_examples`: an example of the source device s. `slot_counts`: slots 0 to count - 1 of a bucket are live, the others unused; some bucket of every draw is full.
All inputs are finite; a program needn't handle non-finite values.
Results may differ from a plain program's by a relative error of at most 0.0003.
Values sent between devices are 32-bit elements; how exact they have to be, the bound alone decides.
A program may use at most 64 MiB of HBM per device.

v0:
```python
import functools

import jax
import jax.numpy as jnp
from jax import lax
from jax.experimental import pallas as pl
from jax.experimental.pallas import tpu as pltpu
from jax.sharding import PartitionSpec as P

MESH = pl.DeviceIdType.MESH
CHUNKS = 2
DEAD = -65536


def kernel(
    n,
    cols,
    tables_hbm,
    dense_hbm,
    rows_hbm,
    examples_hbm,
    counts_hbm,
    pooled_ref,
    inter_ref,
    dense_ref,
    rows_ref,
    examples_ref,
    counts_ref,
    table_buf,
    split_buf,
    id_send,
    id_recv,
    pair_keep,
    pair_send,
    pair_recv,
    far_send,
    far_recv,
    near_recv,
    gram_recv,
    gram_send,
    load_sem,
    id_ssem,
    id_rsem,
    pair_ssem,
    pair_rsem,
    far_ssem,
    far_rsem,
    near_ssem,
    near_rsem,
    gram_ssem,
    gram_rsem,
):
    tables, range_rows, width = table_buf.shape
    here = dense_ref.shape[0]
    cap = rows_ref.shape[3]
    far = n // 2
    chunks = pair_ssem.shape[1]
    step = tables // chunks
    me = lax.axis_index("rows")
    col = lax.axis_index("cols")
    hi, lo = me // 2, me % 2
    mate = hi * 2 + (1 - lo)

    sources = (counts_hbm, rows_hbm, examples_hbm, tables_hbm, dense_hbm)
    targets = (counts_ref, rows_ref, examples_ref, table_buf, dense_ref)
    loads = [pltpu.make_async_copy(a, b, load_sem.at[i]) for i, (a, b) in enumerate(zip(sources, targets))]

    barrier = pltpu.get_barrier_semaphore()
    for j in range(1, n):
        pl.semaphore_signal(barrier, inc=1, device_id={"rows": (me + j) % n}, device_id_type=MESH)
    for j in range(1, cols):
        pl.semaphore_signal(barrier, inc=1, device_id={"cols": (col + j) % cols}, device_id_type=MESH)

    for load in loads:
        load.start()

    slot = lax.broadcasted_iota(jnp.int32, (tables, cap), 1)
    table_id = lax.broadcasted_iota(jnp.int32, (tables, cap), 0)
    for load in loads[:3]:
        load.wait()
    for p in range(n):
        count = jnp.full((tables, cap), counts_ref[0, 0, p], jnp.int32)
        for t in range(1, tables):
            count = jnp.where(table_id == t, counts_ref[0, t, p], count)
        rows_p = rows_ref[0, p]
        ex_p = jnp.where(slot < count, examples_ref[0, p], DEAD)
        id_send[p, 0:tables, :] = jnp.concatenate([rows_p, rows_p], axis=1)
        id_send[p, tables : 2 * tables, :] = jnp.concatenate([ex_p, ex_p], axis=1)

    pl.semaphore_wait(barrier, n - 1 + cols - 1)

    def group_of(k):
        return (hi // 2 + 1 + k // 2) % (far // 2) * 2 + (hi + 1 + k) % 2

    def id_copy(dst):
        return pltpu.make_async_remote_copy(
            src_ref=id_send.at[dst],
            dst_ref=id_recv.at[me],
            send_sem=id_ssem.at[dst],
            recv_sem=id_rsem.at[me],
            device_id={"rows": dst},
            device_id_type=MESH,
        )

    def id_wait(src):
        pltpu.make_async_remote_copy(
            src_ref=id_send.at[src],
            dst_ref=id_recv.at[src],
            send_sem=id_ssem.at[src],
            recv_sem=id_rsem.at[src],
            device_id={"rows": src},
            device_id_type=MESH,
        ).wait_recv()

    for k in range(far - 1):
        dst_hi = group_of(k)
        id_copy(dst_hi * 2 + lo).start()
        id_copy(dst_hi * 2 + (1 - lo)).start()
    id_copy(mate).start()
    id_recv[me] = id_send[me]

    loads[3].wait()
    for t in range(tables):
        whole = table_buf[t]
        high = whole.astype(jnp.bfloat16)
        split_buf[t, :, 0:width] = high
        split_buf[t, :, width : 2 * width] = (whole - high.astype(jnp.float32)).astype(jnp.bfloat16)

    first_half = lax.broadcasted_iota(jnp.int32, (tables, 2 * cap), 1) < cap
    offset = jnp.where(first_half, lo * here, (1 - lo) * here)
    row_iota = lax.broadcasted_iota(jnp.int32, (range_rows, 2 * cap), 0)
    ex_iota = lax.broadcasted_iota(jnp.int32, (2 * here, 2 * cap), 0)

    def pair_copy(g, c):
        piece = pl.ds(c * step, step)
        return pltpu.make_async_remote_copy(
            src_ref=pair_send.at[g, piece],
            dst_ref=pair_recv.at[g, piece],
            send_sem=pair_ssem.at[g, c],
            recv_sem=pair_rsem.at[g, c],
            device_id={"rows": mate},
            device_id_type=MESH,
        )

    def far_copy(g, c):
        piece = pl.ds(c * step, step)
        return pltpu.make_async_remote_copy(
            src_ref=far_send.at[g, piece],
            dst_ref=far_recv.at[hi, piece],
            send_sem=far_ssem.at[g, c],
            recv_sem=far_rsem.at[hi, c],
            device_id={"rows": g * 2 + lo},
            device_id_type=MESH,
        )

    def far_wait(g, c):
        piece = pl.ds(c * step, step)
        pltpu.make_async_remote_copy(
            src_ref=far_send.at[g, piece],
            dst_ref=far_recv.at[g, piece],
            send_sem=far_ssem.at[g, c],
            recv_sem=far_rsem.at[g, c],
            device_id={"rows": g * 2 + lo},
            device_id_type=MESH,
        ).wait_recv()

    near = hi + 1 - 2 * (hi % 2)

    def near_copy(same):
        return pltpu.make_async_remote_copy(
            src_ref=pair_keep.at[near] if same else pair_send.at[near],
            dst_ref=near_recv.at[0 if same else 1],
            send_sem=near_ssem.at[0 if same else 1],
            recv_sem=near_rsem.at[0 if same else 1],
            device_id={"rows": near * 2 + (lo if same else 1 - lo)},
            device_id_type=MESH,
        )

    def compute(g, paired=True):
        even = id_recv[g * 2]
        odd = id_recv[g * 2 + 1]
        row_of = jnp.where(first_half, even[0:tables], odd[0:tables])
        code = jnp.where(first_half, even[tables : 2 * tables], odd[tables : 2 * tables]) + offset
        for t in range(tables):
            row_hot = jnp.where(row_iota == row_of[t : t + 1], 1.0, 0.0).astype(jnp.bfloat16)
            ex_hot = jnp.where(ex_iota == code[t : t + 1], 1.0, 0.0).astype(jnp.bfloat16)
            hits = lax.dot_general(
                ex_hot, row_hot, (((1,), (1,)), ((), ())), preferred_element_type=jnp.float32
            ).astype(jnp.bfloat16)
            both = jnp.dot(hits, split_buf[t], preferred_element_type=jnp.float32)
            part = both[:, 0:width] + both[:, width : 2 * width]
            pair_keep[g, t] = part[0:here]
            pair_send[g, t] = part[here : 2 * here]
            if paired and (t + 1) % step == 0:
                pair_copy(g, t // step).start()

    def forward(g):
        for c in range(chunks):
            pair_copy(g, c).wait_recv()
            piece = pl.ds(c * step, step)
            far_send[g, piece] = pair_keep[g, piece] + pair_recv[g, piece]
            far_copy(g, c).start()

    def remote_group(g):
        id_wait(g * 2)
        id_wait(g * 2 + 1)
        compute(g)

    remote_group(group_of(0))
    if far <= 8:
        for k in range(1, far - 2):
            remote_group(group_of(k))
            forward(group_of(k - 1))
    else:

        @pl.loop(1, far - 2)
        def _(k):
            remote_group(group_of(k))
            forward(group_of(k - 1))

    id_wait(near * 2)
    id_wait(near * 2 + 1)
    compute(near, False)
    near_copy(True).start()
    near_copy(False).start()
    forward(group_of(far - 3))
    id_wait(mate)
    compute(hi)

    for c in range(chunks):
        pair_copy(hi, c).wait_recv()
    total = pair_keep[hi] + pair_recv[hi]
    for same in (True, False):
        near_copy(same).wait_recv()
    total = total + (near_recv[0] + near_recv[1])
    for k in range(far - 2):
        g = group_of(far - 3 - k)
        for c in range(chunks):
            far_wait(g, c)
        total = total + far_recv[g]

    for t in range(tables):
        pooled_ref[:, t, :] = total[t]
    loads[4].wait()
    vectors = [dense_ref[...]] + [total[t] for t in range(tables)]
    lane = lax.broadcasted_iota(jnp.int32, (here, 128), 1)
    gram = jnp.zeros((here, 128), jnp.float32)
    pair = 0
    for i in range(tables + 1):
        for j in range(i + 1, tables + 1):
            inner = jnp.sum(vectors[i] * vectors[j], axis=1, keepdims=True)
            gram = jnp.where(lane == pair, inner, gram)
            pair += 1
    gram = gram.T[0 : gram_send.shape[0]]
    gram_send[...] = gram
    gram_recv[col] = gram

    def gram_copy(j):
        return pltpu.make_async_remote_copy(
            src_ref=gram_send,
            dst_ref=gram_recv.at[col],
            send_sem=gram_ssem.at[j],
            recv_sem=gram_rsem.at[col],
            device_id={"cols": (col + j) % cols},
            device_id_type=MESH,
        )

    for j in range(1, cols):
        gram_copy(j).start()
    for j in range(1, cols):
        src = (col + j) % cols
        pltpu.make_async_remote_copy(
            src_ref=gram_send,
            dst_ref=gram_recv.at[src],
            send_sem=gram_ssem.at[j],
            recv_sem=gram_rsem.at[src],
            device_id={"cols": src},
            device_id_type=MESH,
        ).wait_recv()
    summed = gram_recv[0]
    for c in range(1, cols):
        summed = summed + gram_recv[c]
    inter_ref[...] = (summed * (width * cols) ** (-0.5))[0:pair]

    for j in range(1, n):
        id_copy((me + j) % n).wait_send()
    for c in range(chunks):
        pair_copy(hi, c).wait_send()
        for k in range(far - 2):
            pair_copy(group_of(k), c).wait_send()
            far_copy(group_of(k), c).wait_send()
    for same in (True, False):
        near_copy(same).wait_send()
    for j in range(1, cols):
        gram_copy(j).wait_send()


def body(n, cols, tables, dense_features, slot_rows, slot_examples, slot_counts):
    count, range_rows, width = tables.shape
    here = dense_features.shape[0]
    cap = slot_rows.shape[3]
    far = n // 2
    pairs = (count + 1) * count // 2
    vmem = pl.BlockSpec(memory_space=pltpu.VMEM)
    block = (far, count, here, width)
    chunks = CHUNKS
    any_space = pl.BlockSpec(memory_space=pl.ANY)
    pair_rows = -(-pairs // 8) * 8
    pooled, inter = pl.pallas_call(
        functools.partial(kernel, n, cols),
        out_shape=(
            pltpu.VMEM((here, count, width), jnp.float32),
            pltpu.VMEM((pairs, here), jnp.float32),
        ),
        in_specs=[any_space] * 5,
        out_specs=(vmem, vmem),
        scratch_shapes=[
            pltpu.VMEM((here, width), jnp.float32),
            pltpu.VMEM(slot_rows.shape, jnp.int32),
            pltpu.VMEM(slot_rows.shape, jnp.int32),
            pltpu.SMEM((1, count, n), jnp.int32),
            pltpu.VMEM((count, range_rows, width), jnp.float32),
            pltpu.VMEM((count, range_rows, 2 * width), jnp.bfloat16),
            pltpu.VMEM((n, 2 * count, 2 * cap), jnp.int32),
            pltpu.VMEM((n, 2 * count, 2 * cap), jnp.int32),
            pltpu.VMEM(block, jnp.float32),
            pltpu.VMEM(block, jnp.float32),
            pltpu.VMEM(block, jnp.float32),
            pltpu.VMEM(block, jnp.float32),
            pltpu.VMEM(block, jnp.float32),
            pltpu.VMEM((2,) + block[1:], jnp.float32),
            pltpu.VMEM((cols, pair_rows, here), jnp.float32),
            pltpu.VMEM((pair_rows, here), jnp.float32),
            pltpu.SemaphoreType.DMA((5,)),
            pltpu.SemaphoreType.DMA((n,)),
            pltpu.SemaphoreType.DMA((n,)),
            pltpu.SemaphoreType.DMA((far, chunks)),
            pltpu.SemaphoreType.DMA((far, chunks)),
            pltpu.SemaphoreType.DMA((far, chunks)),
            pltpu.SemaphoreType.DMA((far, chunks)),
            pltpu.SemaphoreType.DMA((2,)),
            pltpu.SemaphoreType.DMA((2,)),
            pltpu.SemaphoreType.DMA((cols,)),
            pltpu.SemaphoreType.DMA((cols,)),
        ],
        compiler_params=pltpu.CompilerParams(collective_id=0, has_side_effects=True),
    )(tables, dense_features, slot_rows, slot_examples, slot_counts.transpose(0, 2, 1))
    return pooled, inter.T


def solution(mesh):
    placed = (
        P(None, "rows", "cols"),
        P("rows", "cols"),
        P("rows", None, None, None),
        P("rows", None, None, None),
        P("rows", None, None),
    )
    return jax.shard_map(
        functools.partial(body, mesh.shape["rows"], mesh.shape["cols"]),
        mesh=mesh,
        in_specs=placed,
        out_specs=(P("rows", None, "cols"), P("rows", None)),
        check_vma=False,
    )
```

profile of v0, /device:TPU:0, one launch (start us, length us, event | category | flops | bytes accessed | tf_op | source)
XLA Modules:
  0.0 24.1 jit_solution(15082893923466095381)
XLA Ops:
  0.6 22.2 %shard_map.68 = (f32[32,4,128]{2,1,0:T(4,128)S(1)}, f32[10,32]{1,0:T(8,128)S(1)}) custom-call(f32[4,512,128]{2,1,0:T(8,128)} %tables_hbm.1, f32[32,128]{1,0:T(8,128)} %dense_hbm.1, s32[1,8,4,64]{3,2,1,0:T(4,128)} %rows_hbm.1, s32[1,8,4,64]{3,2,1,0:T(4,128)} %examples_hbm.1, s32[1,4,8]{2,1,0:T(4,128)} %bitcast.3), custom_call_target="tpu_custom_call" | custom-call | tf_op jit(solution)/shard_map/pallas_call | solution.py:309
  22.8 0.6 %copy.9 = f32[32,4,128]{2,1,0:T(4,128)} copy(f32[32,4,128]{2,1,0:T(4,128)S(1)} %get-tuple-element.6) | data formatting | bytes 131072
  23.5 0.6 %copy.10 = f32[32,10]{0,1:T(8,128)} copy(f32[32,10]{0,1:T(8,128)S(1)} %bitcast.2) | data formatting | bytes 2560
where the time goes:
time: 24.2 us; the launch traced here: 24.1 us
  Pallas kernels  22.2 us (92%)
  local copies, waits for them, and re-layouts  1.23 us (5%)
  between operations  0.64 us (3%)
    pallas_call x1, Pallas kernels, body(): pl.pallas_call(functools.partial(kernel, n, cols), out_shape=(pltpu.VMEM(...  22.2 us
    unnamed x2, local copies, waits for them, and re-layouts  1.23 us

commit v1 on v0

--- a/solution.py
+++ b/solution.py
@@ -345,6 +345,33 @@
         ],
         compiler_params=pltpu.CompilerParams(collective_id=0, has_side_effects=True),
     )(tables, dense_features, slot_rows, slot_examples, slot_counts.transpose(0, 2, 1))
+    return write_out(pooled, inter)
+
+
+def store(pooled_ref, inter_ref, pooled_hbm, inter_hbm, sem):
+    copies = [
+        pltpu.make_async_copy(pooled_ref, pooled_hbm, sem.at[0]),
+        pltpu.make_async_copy(inter_ref, inter_hbm, sem.at[1]),
+    ]
+    for copy in copies:
+        copy.start()
+    for copy in copies:
+        copy.wait()
+
+
+def write_out(pooled, inter):
+    vmem = pl.BlockSpec(memory_space=pltpu.VMEM)
+    hbm = pl.BlockSpec(memory_space=pl.ANY)
+    pooled, inter = pl.pallas_call(
+        store,
+        out_shape=(
+            jax.ShapeDtypeStruct(pooled.shape, pooled.dtype),
+            jax.ShapeDtypeStruct(inter.shape, inter.dtype),
+        ),
+        in_specs=[vmem, vmem],
+        out_specs=(hbm, hbm),
+        scratch_shapes=[pltpu.SemaphoreType.DMA((2,))],
+    )(*(pltpu.with_memory_space_constraint(x, pltpu.VMEM) for x in (pooled, inter)))
     return pooled, inter.T
 
 

time: 24.2 us -> 23.7 us (0.979)
  local copies, waits for them, and re-layouts: 1.23 us -> 0 us
  Pallas kernels: 22.2 us -> 22.9 us
    unnamed x2 -> x0, local copies, waits for them, and re-layouts: 1.23 us -> none
    pallas_call x0 -> x1, Pallas kernels: none -> 0.65 us  [write_out(): pl.pallas_call(store, out_shape=(jax.ShapeDtypeStruct(pooled.shape, poole...]
where the time goes in v1:
time: 23.7 us; the launch traced here: 23.5 us
  Pallas kernels  22.9 us (97%)
  between operations  0.64 us (3%)
    pallas_call x1, Pallas kernels, body(): pl.pallas_call(functools.partial(kernel, n, cols), out_shape=(pltpu.VMEM(...  22.2 us
    pallas_call x1, Pallas kernels, write_out(): pl.pallas_call(store, out_shape=(jax.ShapeDtypeStruct(pooled.shape, poole...  0.65 us

profile of v1, /device:TPU:0, one launch (start us, length us, event | category | flops | bytes accessed | tf_op | source)
XLA Modules:
  0.0 23.5 jit_solution(2717853292879492206)
XLA Ops:
  0.6 22.2 %shard_map.68 = (f32[32,4,128]{2,1,0:T(4,128)S(1)}, f32[10,32]{1,0:T(8,128)S(1)}) custom-call(f32[4,512,128]{2,1,0:T(8,128)} %tables_hbm.1, f32[32,128]{1,0:T(8,128)} %dense_hbm.1, s32[1,8,4,64]{3,2,1,0:T(4,128)} %rows_hbm.1, s32[1,8,4,64]{3,2,1,0:T(4,128)} %examples_hbm.1, s32[1,4,8]{2,1,0:T(4,128)} %bitcast.2), custom_call_target="tpu_custom_call" | custom-call | tf_op jit(solution)/shard_map/pallas_call | solution.py:309
  22.8 0.7 %shard_map.69 = (f32[32,4,128]{2,1,0:T(4,128)}, f32[10,32]{1,0:T(8,128)}) custom-call(f32[32,4,128]{2,1,0:T(4,128)S(1)} %get-tuple-element.6.pooled_ref, f32[10,32]{1,0:T(8,128)S(1)} %get-tuple-element.7.inter_ref), custom_call_target="tpu_custom_call" | custom-call | tf_op jit(solution)/shard_map/pallas_call | solution.py:365

commit v2 on v0

v2 whole, which is shorter than its diff:
```python
import functools

import jax
import jax.numpy as jnp
from jax import lax
from jax.experimental import pallas as pl
from jax.experimental.pallas import tpu as pltpu
from jax.sharding import PartitionSpec as P

MESH = pl.DeviceIdType.MESH
CHUNKS = 2
DEAD = -65536
OWN, DIRECT, PAIR, FORWARD = range(4)
PLANS = {
    4: (
        ((OWN, 0), (PAIR, 2), (DIRECT, 3), (DIRECT, 1), (FORWARD, 2)),
        ((DIRECT, 0), (OWN, 1), (PAIR, 2), (PAIR, 3), (FORWARD, 2), (FORWARD, 3)),
        ((OWN, 2), (PAIR, 0), (PAIR, 1), (DIRECT, 3), (FORWARD, 0), (FORWARD, 1)),
        ((OWN, 3), (DIRECT, 0), (PAIR, 1), (DIRECT, 2), (FORWARD, 1)),
    )
}
ARRIVALS = {4: ((1, 2, 3), (0, 2, 3), (3, 0, 1), (2, 0, 1))}


def repeat(first, last, step, body):
    if (last - first) // step <= 16:
        for k in range(first, last, step):
            body(k)
    else:
        pl.loop(first, last, step=step)(body)


def kernel(
    n,
    cols,
    fan,
    tables_hbm,
    dense_hbm,
    rows_hbm,
    examples_hbm,
    counts_hbm,
    pooled_ref,
    inter_ref,
    dense_ref,
    rows_ref,
    examples_ref,
    counts_ref,
    table_buf,
    split_buf,
    id_send,
    id_recv,
    id_relay,
    keep,
    cross,
    pair_recv,
    far_send,
    data_recv,
    total_ref,
    gram_recv,
    gram_send,
    load_sem,
    id_ssem,
    id_rsem,
    relay_rsem,
    pair_rsem,
    data_ssem,
    data_rsem,
    gram_ssem,
    gram_rsem,
):
    tables, range_rows, width = table_buf.shape
    here = dense_ref.shape[0]
    cap = rows_ref.shape[3]
    far = n // 2
    chunks = pair_rsem.shape[1]
    step = tables // chunks
    me = lax.axis_index("rows")
    col = lax.axis_index("cols")
    hi, lo = me // 2, me % 2
    mate = hi * 2 + (1 - lo)
    near = hi + 1 - 2 * (hi % 2)
    lead = col // fan * fan + fan - 1
    leads = col == lead

    sources = (counts_hbm, rows_hbm, examples_hbm, tables_hbm, dense_hbm)
    targets = (counts_ref, rows_ref, examples_ref, table_buf, dense_ref)
    loads = [pltpu.make_async_copy(a, b, load_sem.at[i]) for i, (a, b) in enumerate(zip(sources, targets))]

    barrier = pltpu.get_barrier_semaphore()

    def greet(row, at):
        pl.semaphore_signal(barrier, inc=1, device_id={"rows": row, "cols": at}, device_id_type=MESH)

    base = jnp.where(hi == 0, 0, me - 2)

    @pl.when(hi == 0)
    def _():
        greet(2, lead)
        greet(mate, lead)

    repeat(1, n - 2, 1, lambda j: greet(2 + (base + j) % (n - 2), lead))

    @pl.when(jnp.logical_and(hi == 1, leads))
    def _():
        greet(0, col)
        greet(1, col)
        for f in range(1, fan):
            greet(mate, lead - f)

    greet(mate, col)
    for j in range(1, cols):
        greet(me, (col + j) % cols)

    for load in loads:
        load.start()

    slot = lax.broadcasted_iota(jnp.int32, (tables, cap), 1)
    table_id = lax.broadcasted_iota(jnp.int32, (tables, cap), 0)
    for load in loads[:3]:
        load.wait()

    def pack(ref, q, p):
        count = jnp.full((tables, cap), counts_ref[0, 0, p], jnp.int32)
        for t in range(1, tables):
            count = jnp.where(table_id == t, counts_ref[0, t, p], count)
        rows_p = rows_ref[0, p]
        ex_p = jnp.where(slot < count, examples_ref[0, p], DEAD)
        ref[q, 0:tables, :] = jnp.concatenate([rows_p, rows_p], axis=1)
        ref[q, tables : 2 * tables, :] = jnp.concatenate([ex_p, ex_p], axis=1)

    @pl.when(leads)
    def _():
        repeat(0, n, 1, lambda p: pack(id_send, p, p))

    if fan > 1:

        @pl.when(jnp.logical_and(jnp.logical_not(leads), hi == 1))
        def _():
            pack(id_send, mate, mate)

    pack(id_recv, me, me)

    loads[3].wait()
    for t in range(tables):
        whole = table_buf[t]
        high = whole.astype(jnp.bfloat16)
        split_buf[t, :, 0:width] = high
        split_buf[t, :, width : 2 * width] = (whole - high.astype(jnp.float32)).astype(jnp.bfloat16)

    first_half = lax.broadcasted_iota(jnp.int32, (tables, 2 * cap), 1) < cap
    offset = jnp.where(first_half, lo * here, (1 - lo) * here)
    row_iota = lax.broadcasted_iota(jnp.int32, (range_rows, 2 * cap), 0)
    ex_iota = lax.broadcasted_iota(jnp.int32, (2 * here, 2 * cap), 0)

    greeted_lead = jnp.where(hi == 0, cols + fan + 2, cols + fan * (n - 1))
    greeted_rest = jnp.where(hi == 1, cols + 1, cols)
    pl.semaphore_wait(barrier, jnp.where(leads, greeted_lead, greeted_rest))

    def id_copy(src, source, row, at, sem):
        return pltpu.make_async_remote_copy(
            src_ref=src,
            dst_ref=id_recv.at[source],
            send_sem=id_ssem.at[sem],
            recv_sem=id_rsem.at[source],
            device_id={"rows": row, "cols": at},
            device_id_type=MESH,
        )

    def id_wait(source):
        id_copy(id_send.at[source], source, source, lead, 0).wait_recv()

    def relay_copy():
        block = pl.ds(4, n - 4)
        return pltpu.make_async_remote_copy(
            src_ref=id_send.at[block],
            dst_ref=id_relay,
            send_sem=id_ssem.at[2 * fan],
            recv_sem=relay_rsem.at[0],
            device_id={"rows": 2 + lo, "cols": lead},
            device_id_type=MESH,
        )

    def mate_ids(buf, q):
        for f in range(fan):
            id_copy(buf.at[q], me, mate, lead - f, f).start()

    def far_ids():
        def send(j):
            row = (hi + j // 2) % far * 2 + (lo + j) % 2
            for f in reversed(range(fan)):
                id_copy(id_send.at[row], me, row, lead - f, f).start()

        repeat(2, n, 1, send)

    @pl.when(jnp.logical_and(leads, hi == 0))
    def _():
        if n > 4:
            relay_copy().start()
        for row in (2, 3):
            id_copy(id_send.at[row], me, row, lead, 2 * fan).start()
        mate_ids(id_send, mate)

    if fan > 1:

        @pl.when(jnp.logical_and(jnp.logical_not(leads), hi == 1))
        def _():
            mate_ids(id_send, mate)

    @pl.when(jnp.logical_and(leads, hi == 1))
    def _():
        if n > 4:
            relay_copy().wait_recv()

            def relay(j):
                row = n + 3 - j
                for f in reversed(range(fan)):
                    id_copy(id_relay.at[row - 4], lo, row, lead - f, fan + f).start()

            repeat(4, n, 1, relay)
        if fan == 1:
            mate_ids(id_send, mate)
        far_ids()
        for source in (0, 1):
            id_wait(source)
            for f in range(1, fan):
                id_copy(id_recv.at[source], source, me, lead - f, 2 * fan).start()

    @pl.when(jnp.logical_and(leads, hi >= 2))
    def _():
        mate_ids(id_send, mate)
        far_ids()

    def send_block(buf, g, piece, row):
        return pltpu.make_async_remote_copy(
            src_ref=buf.at[g, piece],
            dst_ref=data_recv.at[me, piece],
            send_sem=data_ssem.at[0],
            recv_sem=data_rsem.at[me],
            device_id={"rows": row},
            device_id_type=MESH,
        )

    def data_wait(row):
        pltpu.make_async_remote_copy(
            src_ref=data_recv.at[row],
            dst_ref=data_recv.at[row],
            send_sem=data_ssem.at[0],
            recv_sem=data_rsem.at[row],
            device_id={"rows": row},
            device_id_type=MESH,
        ).wait_recv()

    def pair_copy(g, c):
        piece = pl.ds(c * step, step)
        return pltpu.make_async_remote_copy(
            src_ref=cross.at[g, piece],
            dst_ref=pair_recv.at[g, piece],
            send_sem=data_ssem.at[0],
            recv_sem=pair_rsem.at[g, c],
            device_id={"rows": mate},
            device_id_type=MESH,
        )

    def compute(g, then):
        even = id_recv[g * 2]
        odd = id_recv[g * 2 + 1]
        row_of = jnp.where(first_half, even[0:tables], odd[0:tables])
        code = jnp.where(first_half, even[tables : 2 * tables], odd[tables : 2 * tables]) + offset
        hits = []
        for t in range(tables):
            row_hot = jnp.where(row_iota == row_of[t : t + 1], 1.0, 0.0).astype(jnp.bfloat16)
            ex_hot = jnp.where(ex_iota == code[t : t + 1], 1.0, 0.0).astype(jnp.bfloat16)
            hits.append(
                lax.dot_general(
                    ex_hot, row_hot, (((1,), (1,)), ((), ())), preferred_element_type=jnp.float32
                ).astype(jnp.bfloat16)
            )
        for t in range(tables):
            both = jnp.dot(hits[t], split_buf[t], preferred_element_type=jnp.float32)
            part = both[:, 0:width] + both[:, width : 2 * width]
            keep[g, t] = part[0:here]
            cross[g, t] = part[here : 2 * here]
            if (t + 1) % step == 0:
                then(g, t // step)

    def direct(g, c):
        send_block(keep, g, pl.ds(c * step, step), g * 2 + lo).start()
        send_block(cross, g, pl.ds(c * step, step), g * 2 + 1 - lo).start()

    def own(g, c):
        send_block(cross, g, pl.ds(c * step, step), mate).start()

    def paired(g, c):
        pair_copy(g, c).start()

    def forward(g):
        for c in range(chunks):
            pair_copy(g, c).wait_recv()
            piece = pl.ds(c * step, step)
            far_send[g, piece] = keep[g, piece] + pair_recv[g, piece]
            send_block(far_send, g, piece, g * 2 + lo).start()

    def ids_of(g, hub=False):
        if hub:

            @pl.when(jnp.logical_not(leads))
            def _():
                id_wait(0)
                id_wait(1)
        else:
            id_wait(g * 2)
            id_wait(g * 2 + 1)

    def own_group(g):
        id_wait(mate)
        compute(g, own)

    def group(g, then):
        ids_of(g)
        compute(g, then)

    def add_both(g):
        data_wait(g * 2)
        data_wait(g * 2 + 1)
        total_ref[...] += data_recv[g * 2] + data_recv[g * 2 + 1]

    def add_one(g):
        data_wait(g * 2 + lo)
        total_ref[...] += data_recv[g * 2 + lo]

    def planned(r):
        for op, g in PLANS[far][r]:
            if op == OWN:
                own_group(r)
            elif op == FORWARD:
                forward(g)
            else:
                ids_of(g, r == 1 and g == 0)
                compute(g, direct if op == DIRECT else paired)
        data_wait(mate)
        total_ref[...] = keep[r] + data_recv[mate]
        for g in ARRIVALS[far][r]:
            (add_both if (DIRECT, r) in PLANS[far][g] else add_one)(g)

    def others(action):
        def both(m):
            q = (hi // 2 + m) % (far // 2)
            action(q * 2)
            action(q * 2 + 1)

        repeat(1, far // 2, 1, both)

    def general():
        @pl.when(hi != 1)
        def _():
            own_group(hi)
            group(near, direct)

        @pl.when(hi == 1)
        def _():
            ids_of(0, True)
            compute(0, direct)
            own_group(1)

        others(lambda g: group(g, paired))
        others(forward)
        data_wait(mate)
        total_ref[...] = keep[hi] + data_recv[mate]
        add_both(near)
        others(add_one)

    if far in PLANS:
        for r in range(far):
            pl.when(hi == r)(functools.partial(planned, r))
    else:
        general()

    loads[4].wait()
    vectors = [dense_ref[...]] + [total_ref[t] for t in range(tables)]
    lane = lax.broadcasted_iota(jnp.int32, (here, 128), 1)
    gram = jnp.zeros((here, 128), jnp.float32)
    pair = 0
    for i in range(tables + 1):
        for j in range(i + 1, tables + 1):
            inner = jnp.sum(vectors[i] * vectors[j], axis=1, keepdims=True)
            gram = jnp.where(lane == pair, inner, gram)
            pair += 1
    gram = gram.T[0 : gram_send.shape[0]]
    gram_send[...] = gram

    def gram_copy(source, at):
        return pltpu.make_async_remote_copy(
            src_ref=gram_send,
            dst_ref=gram_recv.at[source],
            send_sem=gram_ssem.at[0],
            recv_sem=gram_rsem.at[source],
            device_id={"cols": at},
            device_id_type=MESH,
        )

    for j in range(1, cols):
        gram_copy(col, (col + j) % cols).start()
    gram_recv[col] = gram
    for t in range(tables):
        pooled_ref[:, t, :] = total_ref[t]
    for j in range(1, cols):
        gram_copy((col + j) % cols, col).wait_recv()
    summed = gram_recv[0]
    for c in range(1, cols):
        summed = summed + gram_recv[c]
    inter_ref[...] = (summed * (width * cols) ** (-0.5))[0:pair]

    def sent(ref, sem):
        pltpu.make_async_remote_copy(
            src_ref=ref,
            dst_ref=ref,
            send_sem=sem,
            recv_sem=gram_rsem.at[0],
            device_id={"rows": mate},
            device_id_type=MESH,
        ).wait_send()

    def ids_sent(tiles, sem):
        sent(id_recv.at[pl.ds(0, tiles)], id_ssem.at[sem])

    sent(data_recv.at[pl.ds(0, n - 1)], data_ssem.at[0])
    sent(gram_recv.at[pl.ds(0, cols - 1)], gram_ssem.at[0])

    @pl.when(jnp.logical_and(leads, hi == 0))
    def _():
        for f in range(fan):
            ids_sent(1, f)
        ids_sent(n - 2, 2 * fan)

    @pl.when(jnp.logical_and(leads, hi >= 2))
    def _():
        for f in range(fan):
            ids_sent(n - 1, f)

    if fan > 1:

        @pl.when(jnp.logical_and(jnp.logical_not(leads), hi == 1))
        def _():
            for f in range(fan):
                ids_sent(1, f)

    @pl.when(jnp.logical_and(leads, hi == 1))
    def _():
        for f in range(fan):
            ids_sent(n - 1 if fan == 1 else n - 2, f)
        if n > 4:
            for f in range(fan):
                ids_sent(n - 4, fan + f)
        if fan > 1:
            ids_sent(2 * (fan - 1), 2 * fan)


def store(pooled_ref, inter_ref, pooled_hbm, inter_hbm, sem):
    copies = [
        pltpu.make_async_copy(pooled_ref, pooled_hbm, sem.at[0]),
        pltpu.make_async_copy(inter_ref, inter_hbm, sem.at[1]),
    ]
    for copy in copies:
        copy.start()
    for copy in copies:
        copy.wait()


def write_out(pooled, inter):
    vmem = pl.BlockSpec(memory_space=pltpu.VMEM)
    hbm = pl.BlockSpec(memory_space=pl.ANY)
    pooled, inter = pl.pallas_call(
        store,
        out_shape=(
            jax.ShapeDtypeStruct(pooled.shape, pooled.dtype),
            jax.ShapeDtypeStruct(inter.shape, inter.dtype),
        ),
        in_specs=[vmem, vmem],
        out_specs=(hbm, hbm),
        scratch_shapes=[pltpu.SemaphoreType.DMA((2,))],
    )(*(pltpu.with_memory_space_constraint(x, pltpu.VMEM) for x in (pooled, inter)))
    return pooled, inter.T


def body(n, cols, tables, dense_features, slot_rows, slot_examples, slot_counts):
    count, range_rows, width = tables.shape
    here = dense_features.shape[0]
    cap = slot_rows.shape[3]
    far = n // 2
    fan = 2 if cols % 2 == 0 else 1
    pairs = (count + 1) * count // 2
    vmem = pl.BlockSpec(memory_space=pltpu.VMEM)
    block = (far, count, here, width)
    chunks = CHUNKS
    any_space = pl.BlockSpec(memory_space=pl.ANY)
    pair_rows = -(-pairs // 8) * 8
    tile = (2 * count, 2 * cap)
    pooled, inter = pl.pallas_call(
        functools.partial(kernel, n, cols, fan),
        out_shape=(
            pltpu.VMEM((here, count, width), jnp.float32),
            pltpu.VMEM((pairs, here), jnp.float32),
        ),
        in_specs=[any_space] * 5,
        out_specs=(vmem, vmem),
        scratch_shapes=[
            pltpu.VMEM((here, width), jnp.float32),
            pltpu.VMEM(slot_rows.shape, jnp.int32),
            pltpu.VMEM(slot_rows.shape, jnp.int32),
            pltpu.SMEM((1, count, n), jnp.int32),
            pltpu.VMEM((count, range_rows, width), jnp.float32),
            pltpu.VMEM((count, range_rows, 2 * width), jnp.bfloat16),
            pltpu.VMEM((n,) + tile, jnp.int32),
            pltpu.VMEM((n,) + tile, jnp.int32),
            pltpu.VMEM((max(n - 4, 1),) + tile, jnp.int32),
            pltpu.VMEM(block, jnp.float32),
            pltpu.VMEM(block, jnp.float32),
            pltpu.VMEM(block, jnp.float32),
            pltpu.VMEM(block, jnp.float32),
            pltpu.VMEM((n,) + block[1:], jnp.float32),
            pltpu.VMEM(block[1:], jnp.float32),
            pltpu.VMEM((cols, pair_rows, here), jnp.float32),
            pltpu.VMEM((pair_rows, here), jnp.float32),
            pltpu.SemaphoreType.DMA((5,)),
            pltpu.SemaphoreType.DMA((2 * fan + 1,)),
            pltpu.SemaphoreType.DMA((n,)),
            pltpu.SemaphoreType.DMA((1,)),
            pltpu.SemaphoreType.DMA((far, chunks)),
            pltpu.SemaphoreType.DMA((1,)),
            pltpu.SemaphoreType.DMA((n,)),
            pltpu.SemaphoreType.DMA((1,)),
            pltpu.SemaphoreType.DMA((cols,)),
        ],
        compiler_params=pltpu.CompilerParams(collective_id=0, has_side_effects=True),
    )(tables, dense_features, slot_rows, slot_examples, slot_counts.transpose(0, 2, 1))
    return write_out(pooled, inter)


def solution(mesh):
    placed = (
        P(None, "rows", "cols"),
        P("rows", "cols"),
        P("rows", None, None, None),
        P("rows", None, None, None),
        P("rows", None, None),
    )
    return jax.shard_map(
        functools.partial(body, mesh.shape["rows"], mesh.shape["cols"]),
        mesh=mesh,
        in_specs=placed,
        out_specs=(P("rows", None, "cols"), P("rows", None)),
        check_vma=False,
    )
```

time: 24.2 us -> 21.7 us (0.90); the launches traced: 24.1 us -> 21.3 us
  Pallas kernels: 22.2 us -> 20.6 us
  local copies, waits for them, and re-layouts: 1.23 us -> 0 us
    pallas_call x1 -> x2, Pallas kernels: 22.2 us -> 20.7 us  [the longest x1 20 us: body(): pl.pallas_call(functools.partial(kernel, n, cols, fan), out_shape=(pltpu....]
    unnamed x2 -> x0, local copies, waits for them, and re-layouts: 1.23 us -> none
where the time goes in v2:
time: 21.7 us; the launch traced here: 21.3 us
  Pallas kernels  20.6 us (95%)
  between operations  0.64 us (3%)
    pallas_call x1, Pallas kernels, body(): pl.pallas_call(functools.partial(kernel, n, cols, fan), out_shape=(pltpu....  20 us
    pallas_call x1, Pallas kernels, write_out(): pl.pallas_call(store, out_shape=(jax.ShapeDtypeStruct(pooled.shape, poole...  0.65 us

profile of v2, /device:TPU:0, one launch (start us, length us, event | category | flops | bytes accessed | tf_op | source)
XLA Modules:
  0.0 21.3 jit_solution(417184529150033087)
XLA Ops:
  0.6 20.0 %shard_map.68 = (f32[32,4,128]{2,1,0:T(4,128)S(1)}, f32[10,32]{1,0:T(8,128)S(1)}) custom-call(f32[4,512,128]{2,1,0:T(8,128)} %tables_hbm.1, f32[32,128]{1,0:T(8,128)} %dense_hbm.1, s32[1,8,4,64]{3,2,1,0:T(4,128)} %rows_hbm.1, s32[1,8,4,64]{3,2,1,0:T(4,128)} %examples_hbm.1, s32[1,4,8]{2,1,0:T(4,128)} %bitcast.2), custom_call_target="tpu_custom_call" | custom-call | tf_op jit(solution)/shard_map/pallas_call | solution.py:498
  20.6 0.7 %shard_map.69 = (f32[32,4,128]{2,1,0:T(4,128)}, f32[10,32]{1,0:T(8,128)}) custom-call(f32[32,4,128]{2,1,0:T(4,128)S(1)} %get-tuple-element.6.pooled_ref, f32[10,32]{1,0:T(8,128)S(1)} %get-tuple-element.7.inter_ref), custom_call_target="tpu_custom_call" | custom-call | tf_op jit(solution)/shard_map/pallas_call | solution.py:472

commit v3 on v2

v3 whole, which is shorter than its diff:
```python
import functools

import jax
import jax.numpy as jnp
from jax import lax
from jax.experimental import pallas as pl
from jax.experimental.pallas import tpu as pltpu
from jax.sharding import PartitionSpec as P

MESH = pl.DeviceIdType.MESH
CHUNKS = 4
BLOCKS = 2
DEAD = -65536
OWN, DIRECT, PAIR, MIXED, FORWARD = range(5)
PLANS = {
    4: (
        ((OWN, 0), (PAIR, 2), (MIXED, 3), (DIRECT, 1), (FORWARD, 2), (FORWARD, 3)),
        ((DIRECT, 0), (PAIR, 2), (PAIR, 3), (OWN, 1), (FORWARD, 2), (FORWARD, 3)),
        ((OWN, 2), (PAIR, 0), (PAIR, 1), (DIRECT, 3), (FORWARD, 0), (FORWARD, 1)),
        ((OWN, 3), (DIRECT, 0), (PAIR, 1), (DIRECT, 2), (FORWARD, 1)),
    )
}
ARRIVALS = {4: ((1, 2, 3), (0, 2, 3), (3, 0, 1), (2, 0, 1))}


def repeat(first, last, step, body):
    if (last - first) // step <= 16:
        for k in range(first, last, step):
            body(k)
    else:
        pl.loop(first, last, step=step)(body)


def kernel(
    n,
    cols,
    fan,
    tables_hbm,
    dense_hbm,
    rows_hbm,
    examples_hbm,
    counts_hbm,
    pooled_ref,
    inter_ref,
    dense_ref,
    slots_ref,
    counts_ref,
    table_buf,
    split_buf,
    ids,
    keep,
    cross,
    pair_recv,
    far_send,
    data_recv,
    total_ref,
    gram_recv,
    gram_send,
    load_sem,
    id_ssem,
    id_rsem,
    relay_rsem,
    pair_rsem,
    data_ssem,
    data_rsem,
    gram_ssem,
    gram_rsem,
):
    tables, range_rows, width = table_buf.shape
    here = dense_ref.shape[0]
    cap = slots_ref.shape[4]
    far = n // 2
    chunks = pair_rsem.shape[1]
    step = tables // chunks
    me = lax.axis_index("rows")
    col = lax.axis_index("cols")
    hi, lo = me // 2, me % 2
    mate = hi * 2 + (1 - lo)
    near = hi + 1 - 2 * (hi % 2)
    lead = col // fan * fan + fan - 1
    leads = col == lead
    id_send, id_recv, id_relay = ids.at[pl.ds(0, n)], ids.at[pl.ds(n, n)], ids.at[pl.ds(2 * n, max(n - 4, 1))]
    early = lead - fan + 1

    loads = [
        pltpu.make_async_copy(source, target, load_sem.at[i])
        for source, target, i in (
            (counts_hbm, counts_ref, 0),
            (rows_hbm, slots_ref.at[0], 1),
            (examples_hbm, slots_ref.at[1], 1),
            (tables_hbm, table_buf, 2),
            (dense_hbm, dense_ref, 3),
        )
    ]

    barrier = pltpu.get_barrier_semaphore()

    def greet(row, at):
        pl.semaphore_signal(barrier, inc=1, device_id={"rows": row, "cols": at}, device_id_type=MESH)

    @pl.when(hi == 0)
    def _():
        greet(2, early)
        greet(3, early)
        greet(mate, lead)
        repeat(4, n, 1, lambda row: greet(row, lead))

    @pl.when(hi >= 1)
    def _():
        repeat(1, n - 2, 1, lambda j: greet(2 + (me - 2 + j) % (n - 2), lead))

    @pl.when(jnp.logical_and(hi == 1, leads))
    def _():
        greet(0, col)
        greet(1, col)
        for f in range(1, fan):
            greet(mate, lead - f)

    greet(mate, col)
    for j in range(1, cols):
        greet(me, (col + j) % cols)

    for load in loads:
        load.start()

    slot = lax.broadcasted_iota(jnp.int32, (tables, cap), 1)
    table_id = lax.broadcasted_iota(jnp.int32, (tables, cap), 0)
    loads[0].wait()
    pltpu.make_async_copy(slots_ref, slots_ref, load_sem.at[1]).wait()

    def pack(ref, q, p):
        count = jnp.full((tables, cap), counts_ref[0, 0, p], jnp.int32)
        for t in range(1, tables):
            count = jnp.where(table_id == t, counts_ref[0, t, p], count)
        rows_p = slots_ref[0, 0, p]
        ex_p = jnp.where(slot < count, slots_ref[1, 0, p], DEAD)
        ref[q, 0:tables, :] = jnp.concatenate([rows_p, rows_p], axis=1)
        ref[q, tables : 2 * tables, :] = jnp.concatenate([ex_p, ex_p], axis=1)

    @pl.when(leads)
    def _():
        repeat(0, n, 1, lambda p: pack(id_send, p, p))

    if fan > 1:

        @pl.when(jnp.logical_and(jnp.logical_not(leads), hi == 1))
        def _():
            for row in (mate, 0, 1):
                pack(id_send, row, row)

    pack(id_recv, me, me)

    loads[3].wait()
    for t in range(tables):
        whole = table_buf[t]
        high = whole.astype(jnp.bfloat16)
        split_buf[t, :, 0:width] = high
        split_buf[t, :, width : 2 * width] = (whole - high.astype(jnp.float32)).astype(jnp.bfloat16)

    first_half = lax.broadcasted_iota(jnp.int32, (tables, 2 * cap), 1) < cap
    offset = jnp.where(first_half, lo * here, (1 - lo) * here)
    row_iota = lax.broadcasted_iota(jnp.int32, (range_rows, 2 * cap), 0)
    ex_iota = lax.broadcasted_iota(jnp.int32, (2 * here, 2 * cap), 0)

    greeted_lead = cols + fan * (n - 1)
    greeted_lead = jnp.where(hi == 0, cols + fan + 2, greeted_lead)
    greeted_lead = jnp.where(hi == 1, cols + fan * (n - 3) + (2 if fan == 1 else 0), greeted_lead)
    greeted_rest = jnp.where(hi == 1, cols + 1 + 2 * fan, cols)
    pl.semaphore_wait(barrier, jnp.where(leads, greeted_lead, greeted_rest))

    def id_copy(src, source, row, at):
        return pltpu.make_async_remote_copy(
            src_ref=src,
            dst_ref=id_recv.at[source],
            send_sem=id_ssem.at[0],
            recv_sem=id_rsem.at[source // 2],
            device_id={"rows": row, "cols": at},
            device_id_type=MESH,
        )

    def ids_wait(first, tiles):
        block = id_recv.at[pl.ds(first, tiles)]
        pltpu.make_async_remote_copy(
            src_ref=block,
            dst_ref=block,
            send_sem=id_ssem.at[0],
            recv_sem=id_rsem.at[first // 2],
            device_id={"rows": mate},
            device_id_type=MESH,
        ).wait_recv()

    def relay_copy():
        block = pl.ds(4, n - 4)
        return pltpu.make_async_remote_copy(
            src_ref=id_send.at[block],
            dst_ref=id_relay,
            send_sem=id_ssem.at[0],
            recv_sem=relay_rsem.at[0],
            device_id={"rows": 2 + lo, "cols": lead},
            device_id_type=MESH,
        )

    def ids_to(row):
        for f in reversed(range(fan)):
            id_copy(id_send.at[row], me, row, lead - f).start()

    def far_ids(last):
        repeat(2, last, 1, lambda j: ids_to((hi + j // 2) % far * 2 + (lo + j) % 2))

    @pl.when(jnp.logical_and(leads, hi == 0))
    def _():
        if n > 4:
            relay_copy().start()
        for row in (2, 3):
            id_copy(id_send.at[row], me, row, lead).start()
        ids_to(mate)

    @pl.when(jnp.logical_and(col == early, hi == 1))
    def _():
        for row in (mate, 0, 1):
            ids_to(row)

    @pl.when(jnp.logical_and(leads, hi == 1))
    def _():
        if n > 4:
            relay_copy().wait_recv()

            def relay(j):
                row = n + 3 - j
                for f in reversed(range(fan)):
                    id_copy(id_relay.at[row - 4], lo, row, lead - f).start()

            repeat(4, n, 1, relay)
        far_ids(n - 2)
        ids_wait(0, 2)
        for f in range(1, fan):
            for source in (0, 1):
                id_copy(id_recv.at[source], source, me, lead - f).start()

    @pl.when(jnp.logical_and(leads, hi >= 2))
    def _():
        ids_to(mate)
        far_ids(n)

    def send_block(buf, g, piece, row):
        return pltpu.make_async_remote_copy(
            src_ref=buf.at[g, piece],
            dst_ref=data_recv.at[pl.ds(me * tables + piece.start, piece.size)],
            send_sem=data_ssem.at[0],
            recv_sem=data_rsem.at[hi],
            device_id={"rows": row},
            device_id_type=MESH,
        )

    def slot_of(row):
        return pl.ds(row * tables, tables)

    def data_wait(g, first, blocks):
        block = data_recv.at[pl.ds(first, blocks)]
        pltpu.make_async_remote_copy(
            src_ref=block,
            dst_ref=block,
            send_sem=data_ssem.at[0],
            recv_sem=data_rsem.at[g],
            device_id={"rows": mate},
            device_id_type=MESH,
        ).wait_recv()

    def pair_copy(g, c):
        piece = pl.ds(c * step, step)
        return pltpu.make_async_remote_copy(
            src_ref=cross.at[g, piece],
            dst_ref=pair_recv.at[g, piece],
            send_sem=data_ssem.at[0],
            recv_sem=pair_rsem.at[(g - hi - 1) % far, c],
            device_id={"rows": mate},
            device_id_type=MESH,
        )

    def compute(g, then):
        even = id_recv[g * 2]
        odd = id_recv[g * 2 + 1]
        row_of = jnp.where(first_half, even[0:tables], odd[0:tables])
        code = jnp.where(first_half, even[tables : 2 * tables], odd[tables : 2 * tables]) + offset
        def count(t):
            row_hot = jnp.where(row_iota == row_of[t : t + 1], 1.0, 0.0).astype(jnp.bfloat16)
            ex_hot = jnp.where(ex_iota == code[t : t + 1], 1.0, 0.0).astype(jnp.bfloat16)
            return lax.dot_general(
                ex_hot, row_hot, (((1,), (1,)), ((), ())), preferred_element_type=jnp.float32
            ).astype(jnp.bfloat16)

        def look_up(t, hits):
            both = jnp.dot(hits, split_buf[t], preferred_element_type=jnp.float32)
            return both[:, 0:width] + both[:, width : 2 * width]

        hits = [count(t) for t in range(tables)]
        parts = [look_up(t, hits[t]) for t in range(tables)]
        for t in range(tables):
            keep[g, t] = parts[t][0:here]
            cross[g, t] = parts[t][here : 2 * here]
            if (t + 1) % step == 0:
                then(g, t // step)

    span = tables // BLOCKS

    def pieces(c):
        last = (c + 1) * step
        return [pl.ds(last - span, span)] if last % span == 0 else []

    def direct(g, c):
        for piece in pieces(c):
            send_block(keep, g, piece, g * 2 + lo).start()
            send_block(cross, g, piece, g * 2 + 1 - lo).start()

    def own(g, c):
        for piece in pieces(c):
            send_block(cross, g, piece, mate).start()

    def paired(g, c):
        pair_copy(g, c).start()

    def forward(g, some):
        for c in range(some):
            pair_copy(g, c).wait_recv()
            piece = pl.ds(c * step, step)
            far_send[g, piece] = keep[g, piece] + pair_recv[g, piece]
            send_block(far_send, g, piece, g * 2 + lo).start()

    def mixed(g, c):
        (direct if c >= chunks // 2 else paired)(g, c)

    def ids_of(g, hub=False):
        if hub:
            pl.when(jnp.logical_not(leads))(lambda: ids_wait(g * 2, 2))
        else:
            ids_wait(g * 2, 2)

    def own_group(g):
        ids_wait(mate, 1)
        compute(g, own)

    def add_own(g):
        data_wait(g, mate * tables, tables)
        total_ref[...] = keep[g] + data_recv[slot_of(mate)]

    def add_direct(g):
        data_wait(g, 2 * g * tables, 2 * tables)
        total_ref[...] += data_recv[slot_of(2 * g)] + data_recv[slot_of(2 * g + 1)]

    def add_paired(g):
        data_wait(g, (2 * g + lo) * tables, tables)
        total_ref[...] += data_recv[slot_of(2 * g + lo)]

    def add_mixed(g):
        late = tables // 2
        data_wait(g, 2 * g * tables, tables + late)
        total_ref[...] += data_recv[slot_of(2 * g + lo)]
        total_ref[late:] += data_recv[pl.ds((2 * g + 1 - lo) * tables + late, late)]

    def planned(r):
        sends = {DIRECT: direct, PAIR: paired, MIXED: mixed}
        adds = {DIRECT: add_direct, PAIR: add_paired, MIXED: add_mixed}
        plan = PLANS[far][r]
        for op, g in plan:
            if op == OWN:
                own_group(r)
            elif op == FORWARD:
                forward(g, chunks // 2 if (MIXED, g) in plan else chunks)
            else:
                ids_of(g, r == 1 and g == 0)
                compute(g, sends[op])
        add_own(r)
        for g in ARRIVALS[far][r]:
            adds[next(op for op, to in PLANS[far][g] if op in adds and to == r)](g)

    def others(action):
        def both(m):
            q = (hi // 2 + m) % (far // 2)
            action(q * 2)
            action(q * 2 + 1)

        repeat(1, far // 2, 1, both)

    def general():
        @pl.when(hi != 1)
        def _():
            own_group(hi)
            ids_of(near)
            compute(near, direct)

        @pl.when(hi == 1)
        def _():
            ids_of(0, True)
            compute(0, direct)
            own_group(1)

        def far_group(g):
            ids_of(g)
            compute(g, paired)

        others(far_group)
        others(lambda g: forward(g, chunks))
        add_own(hi)
        add_direct(near)
        others(add_paired)

    if far in PLANS:
        for r in range(far):
            pl.when(hi == r)(functools.partial(planned, r))
    else:
        general()

    loads[4].wait()
    vectors = [dense_ref[...]] + [total_ref[t] for t in range(tables)]
    lane = lax.broadcasted_iota(jnp.int32, (here, 128), 1)
    gram = jnp.zeros((here, 128), jnp.float32)
    pair = 0
    for i in range(tables + 1):
        for j in range(i + 1, tables + 1):
            inner = jnp.sum(vectors[i] * vectors[j], axis=1, keepdims=True)
            gram = jnp.where(lane == pair, inner, gram)
            pair += 1
    gram = gram.T[0 : gram_send.shape[0]]
    gram_send[...] = gram

    def gram_copy(source, at):
        return pltpu.make_async_remote_copy(
            src_ref=gram_send,
            dst_ref=gram_recv.at[source],
            send_sem=gram_ssem.at[0],
            recv_sem=gram_rsem.at[0],
            device_id={"cols": at},
            device_id_type=MESH,
        )

    for j in range(1, cols):
        gram_copy(col, (col + j) % cols).start()
    gram_recv[col] = gram
    for t in range(tables):
        pooled_ref[:, t, :] = total_ref[t]
    block = gram_recv.at[pl.ds(0, cols - 1)]
    pltpu.make_async_remote_copy(
        src_ref=block,
        dst_ref=block,
        send_sem=gram_ssem.at[0],
        recv_sem=gram_rsem.at[0],
        device_id={"rows": mate},
        device_id_type=MESH,
    ).wait_recv()
    summed = gram_recv[0]
    for c in range(1, cols):
        summed = summed + gram_recv[c]
    inter_ref[...] = (summed * (width * cols) ** (-0.5))[0:pair]

    def sent(ref, sem):
        pltpu.make_async_remote_copy(
            src_ref=ref,
            dst_ref=ref,
            send_sem=sem,
            recv_sem=gram_rsem.at[0],
            device_id={"rows": mate},
            device_id_type=MESH,
        ).wait_send()

    sent(data_recv.at[pl.ds(0, (n - 1) * tables)], data_ssem.at[0])
    sent(gram_recv.at[pl.ds(0, cols - 1)], gram_ssem.at[0])

    far_sent = fan * (n - 4)
    hub_sent = far_sent + (far_sent + 2 * (fan - 1) if fan > 1 else n - 1)

    def ids_sent(when, tiles):
        @pl.when(when)
        def _():
            sent(ids.at[pl.ds(0, tiles)], id_ssem.at[0])

    ids_sent(jnp.logical_and(leads, hi == 0), fan + n - 2)
    ids_sent(jnp.logical_and(leads, hi == 1), hub_sent)
    ids_sent(jnp.logical_and(leads, hi >= 2), fan * (n - 1))
    if fan > 1:
        ids_sent(jnp.logical_and(col == early, hi == 1), 3 * fan)


def store(pooled_ref, inter_ref, pooled_hbm, inter_hbm, sem):
    copies = [
        pltpu.make_async_copy(pooled_ref, pooled_hbm, sem.at[0]),
        pltpu.make_async_copy(inter_ref, inter_hbm, sem.at[1]),
    ]
    for copy in copies:
        copy.start()
    for copy in copies:
        copy.wait()


def write_out(pooled, inter):
    vmem = pl.BlockSpec(memory_space=pltpu.VMEM)
    hbm = pl.BlockSpec(memory_space=pl.ANY)
    pooled, inter = pl.pallas_call(
        store,
        out_shape=(
            jax.ShapeDtypeStruct(pooled.shape, pooled.dtype),
            jax.ShapeDtypeStruct(inter.shape, inter.dtype),
        ),
        in_specs=[vmem, vmem],
        out_specs=(hbm, hbm),
        scratch_shapes=[pltpu.SemaphoreType.DMA((2,))],
    )(*(pltpu.with_memory_space_constraint(x, pltpu.VMEM) for x in (pooled, inter)))
    return pooled, inter.T


def body(n, cols, tables, dense_features, slot_rows, slot_examples, slot_counts):
    count, range_rows, width = tables.shape
    here = dense_features.shape[0]
    cap = slot_rows.shape[3]
    far = n // 2
    fan = 2 if cols % 2 == 0 else 1
    pairs = (count + 1) * count // 2
    vmem = pl.BlockSpec(memory_space=pltpu.VMEM)
    block = (far, count, here, width)
    chunks = CHUNKS
    any_space = pl.BlockSpec(memory_space=pl.ANY)
    pair_rows = -(-pairs // 8) * 8
    tile = (2 * count, 2 * cap)
    pooled, inter = pl.pallas_call(
        functools.partial(kernel, n, cols, fan),
        out_shape=(
            pltpu.VMEM((here, count, width), jnp.float32),
            pltpu.VMEM((pairs, here), jnp.float32),
        ),
        in_specs=[any_space] * 5,
        out_specs=(vmem, vmem),
        scratch_shapes=[
            pltpu.VMEM((here, width), jnp.float32),
            pltpu.VMEM((2,) + slot_rows.shape, jnp.int32),
            pltpu.SMEM((1, count, n), jnp.int32),
            pltpu.VMEM((count, range_rows, width), jnp.float32),
            pltpu.VMEM((count, range_rows, 2 * width), jnp.bfloat16),
            pltpu.VMEM((4 * n,) + tile, jnp.int32),
            pltpu.VMEM(block, jnp.float32),
            pltpu.VMEM(block, jnp.float32),
            pltpu.VMEM(block, jnp.float32),
            pltpu.VMEM(block, jnp.float32),
            pltpu.VMEM((n * count,) + block[2:], jnp.float32),
            pltpu.VMEM(block[1:], jnp.float32),
            pltpu.VMEM((cols, pair_rows, here), jnp.float32),
            pltpu.VMEM((pair_rows, here), jnp.float32),
            pltpu.SemaphoreType.DMA((4,)),
            pltpu.SemaphoreType.DMA((1,)),
            pltpu.SemaphoreType.DMA((far,)),
            pltpu.SemaphoreType.DMA((1,)),
            pltpu.SemaphoreType.DMA((far - 1, chunks)),
            pltpu.SemaphoreType.DMA((1,)),
            pltpu.SemaphoreType.DMA((far,)),
            pltpu.SemaphoreType.DMA((1,)),
            pltpu.SemaphoreType.DMA((1,)),
        ],
        compiler_params=pltpu.CompilerParams(collective_id=0, has_side_effects=True),
    )(tables, dense_features, slot_rows, slot_examples, slot_counts.transpose(0, 2, 1))
    return write_out(pooled, inter)


def solution(mesh):
    placed = (
        P(None, "rows", "cols"),
        P("rows", "cols"),
        P("rows", None, None, None),
        P("rows", None, None, None),
        P("rows", None, None),
    )
    return jax.shard_map(
        functools.partial(body, mesh.shape["rows"], mesh.shape["cols"]),
        mesh=mesh,
        in_specs=placed,
        out_specs=(P("rows", None, "cols"), P("rows", None)),
        check_vma=False,
    )
```

time: 21.7 us -> 21.3 us (0.982); the launches traced: 21.3 us -> 21.1 us
  no operation moved by 1% of the time
where the time goes in v3:
time: 21.3 us; the launch traced here: 21.1 us
  Pallas kernels  20.5 us (96%)
  between operations  0.64 us (3%)
    pallas_call x1, Pallas kernels, body(): pl.pallas_call(functools.partial(kernel, n, cols, fan), out_shape=(pltpu....  19.9 us
    pallas_call x1, Pallas kernels, write_out(): pl.pallas_call(store, out_shape=(jax.ShapeDtypeStruct(pooled.shape, poole...  0.65 us

profile of v3, /device:TPU:0, one launch (start us, length us, event | category | flops | bytes accessed | tf_op | source)
XLA Modules:
  0.0 21.1 jit_solution(3915162568547484641)
XLA Ops:
  0.6 19.9 %shard_map.68 = (f32[32,4,128]{2,1,0:T(4,128)S(1)}, f32[10,32]{1,0:T(8,128)S(1)}) custom-call(f32[4,512,128]{2,1,0:T(8,128)} %tables_hbm.1, f32[32,128]{1,0:T(8,128)} %dense_hbm.1, s32[1,8,4,64]{3,2,1,0:T(4,128)} %rows_hbm.1, s32[1,8,4,64]{3,2,1,0:T(4,128)} %examples_hbm.1, s32[1,4,8]{2,1,0:T(4,128)} %bitcast.2), custom_call_target="tpu_custom_call" | custom-call | tf_op jit(solution)/shard_map/pallas_call | solution.py:523
  20.5 0.7 %shard_map.69 = (f32[32,4,128]{2,1,0:T(4,128)}, f32[10,32]{1,0:T(8,128)}) custom-call(f32[32,4,128]{2,1,0:T(4,128)S(1)} %get-tuple-element.6.pooled_ref, f32[10,32]{1,0:T(8,128)S(1)} %get-tuple-element.7.inter_ref), custom_call_target="tpu_custom_call" | custom-call | tf_op jit(solution)/shard_map/pallas_call | solution.py:497

commit v4 on v3

--- a/solution.py
+++ b/solution.py
@@ -11,10 +11,10 @@
 CHUNKS = 4
 BLOCKS = 2
 DEAD = -65536
-OWN, DIRECT, PAIR, MIXED, FORWARD = range(5)
+OWN, DIRECT, PAIR, FORWARD = range(4)
 PLANS = {
     4: (
-        ((OWN, 0), (PAIR, 2), (MIXED, 3), (DIRECT, 1), (FORWARD, 2), (FORWARD, 3)),
+        ((OWN, 0), (PAIR, 2), (PAIR, 3), (DIRECT, 1), (FORWARD, 2), (FORWARD, 3)),
         ((DIRECT, 0), (PAIR, 2), (PAIR, 3), (OWN, 1), (FORWARD, 2), (FORWARD, 3)),
         ((OWN, 2), (PAIR, 0), (PAIR, 1), (DIRECT, 3), (FORWARD, 0), (FORWARD, 1)),
         ((OWN, 3), (DIRECT, 0), (PAIR, 1), (DIRECT, 2), (FORWARD, 1)),
@@ -65,6 +65,7 @@
     data_rsem,
     gram_ssem,
     gram_rsem,
+    ready_sem,
 ):
     tables, range_rows, width = table_buf.shape
     here = dense_ref.shape[0]
@@ -117,13 +118,14 @@
             greet(mate, lead - f)
 
     greet(mate, col)
-    for j in range(1, cols):
-        greet(me, (col + j) % cols)
+    for c in range(1, cols):
+        pl.when(col < c)(functools.partial(greet, me, c))
 
     for load in loads:
         load.start()
 
     slot = lax.broadcasted_iota(jnp.int32, (tables, cap), 1)
+    half = lax.broadcasted_iota(jnp.int32, (tables, 2 * cap), 1) // cap
     table_id = lax.broadcasted_iota(jnp.int32, (tables, cap), 0)
     loads[0].wait()
     pltpu.make_async_copy(slots_ref, slots_ref, load_sem.at[1]).wait()
@@ -134,8 +136,8 @@
             count = jnp.where(table_id == t, counts_ref[0, t, p], count)
         rows_p = slots_ref[0, 0, p]
         ex_p = jnp.where(slot < count, slots_ref[1, 0, p], DEAD)
-        ref[q, 0:tables, :] = jnp.concatenate([rows_p, rows_p], axis=1)
-        ref[q, tables : 2 * tables, :] = jnp.concatenate([ex_p, ex_p], axis=1)
+        rows_p = jnp.concatenate([rows_p, rows_p], axis=1)
+        ref[q] = jnp.where(half == lo, rows_p, jnp.concatenate([ex_p, ex_p], axis=1))
 
     @pl.when(leads)
     def _():
@@ -157,16 +159,19 @@
         split_buf[t, :, 0:width] = high
         split_buf[t, :, width : 2 * width] = (whole - high.astype(jnp.float32)).astype(jnp.bfloat16)
 
-    first_half = lax.broadcasted_iota(jnp.int32, (tables, 2 * cap), 1) < cap
+    first_half = half == 0
     offset = jnp.where(first_half, lo * here, (1 - lo) * here)
     row_iota = lax.broadcasted_iota(jnp.int32, (range_rows, 2 * cap), 0)
     ex_iota = lax.broadcasted_iota(jnp.int32, (2 * here, 2 * cap), 0)
 
-    greeted_lead = cols + fan * (n - 1)
-    greeted_lead = jnp.where(hi == 0, cols + fan + 2, greeted_lead)
-    greeted_lead = jnp.where(hi == 1, cols + fan * (n - 3) + (2 if fan == 1 else 0), greeted_lead)
-    greeted_rest = jnp.where(hi == 1, cols + 1 + 2 * fan, cols)
+    greeted_lead = col + 1 + fan * (n - 1)
+    greeted_lead = jnp.where(hi == 0, col + fan + 3, greeted_lead)
+    greeted_lead = jnp.where(hi == 1, col + 1 + fan * (n - 3) + (2 if fan == 1 else 0), greeted_lead)
+    greeted_rest = jnp.where(hi == 1, col + 2 + 2 * fan, col + 1)
     pl.semaphore_wait(barrier, jnp.where(leads, greeted_lead, greeted_rest))
+
+    def answer(at):
+        pl.semaphore_signal(ready_sem, inc=1, device_id={"cols": at}, device_id_type=MESH)
 
     def id_copy(src, source, row, at):
         return pltpu.make_async_remote_copy(
@@ -204,8 +209,12 @@
         for f in reversed(range(fan)):
             id_copy(id_send.at[row], me, row, lead - f).start()
 
-    def far_ids(last):
-        repeat(2, last, 1, lambda j: ids_to((hi + j // 2) % far * 2 + (lo + j) % 2))
+    def far_ids(first):
+        def to(j):
+            g = j // 2
+            ids_to(jnp.where(g >= hi, g + 1, g) * 2 + (lo + j) % 2)
+
+        repeat(first, n - 2, 1, to)
 
     @pl.when(jnp.logical_and(leads, hi == 0))
     def _():
@@ -231,7 +240,7 @@
                     id_copy(id_relay.at[row - 4], lo, row, lead - f).start()
 
             repeat(4, n, 1, relay)
-        far_ids(n - 2)
+        far_ids(2)
         ids_wait(0, 2)
         for f in range(1, fan):
             for source in (0, 1):
@@ -240,7 +249,10 @@
     @pl.when(jnp.logical_and(leads, hi >= 2))
     def _():
         ids_to(mate)
-        far_ids(n)
+        far_ids(0)
+
+    for c in range(cols - 1):
+        pl.when(col > c)(functools.partial(answer, c))
 
     def send_block(buf, g, piece, row):
         return pltpu.make_async_remote_copy(
@@ -280,8 +292,9 @@
     def compute(g, then):
         even = id_recv[g * 2]
         odd = id_recv[g * 2 + 1]
-        row_of = jnp.where(first_half, even[0:tables], odd[0:tables])
-        code = jnp.where(first_half, even[tables : 2 * tables], odd[tables : 2 * tables]) + offset
+        row_of = jnp.where(first_half, even, odd)
+        code = jnp.where(first_half, odd, even)
+        code = jnp.concatenate([code[:, cap:], code[:, :cap]], axis=1) + offset
         def count(t):
             row_hot = jnp.where(row_iota == row_of[t : t + 1], 1.0, 0.0).astype(jnp.bfloat16)
             ex_hot = jnp.where(ex_iota == code[t : t + 1], 1.0, 0.0).astype(jnp.bfloat16)
@@ -319,15 +332,12 @@
     def paired(g, c):
         pair_copy(g, c).start()
 
-    def forward(g, some):
-        for c in range(some):
+    def forward(g):
+        for c in range(chunks):
             pair_copy(g, c).wait_recv()
             piece = pl.ds(c * step, step)
             far_send[g, piece] = keep[g, piece] + pair_recv[g, piece]
             send_block(far_send, g, piece, g * 2 + lo).start()
-
-    def mixed(g, c):
-        (direct if c >= chunks // 2 else paired)(g, c)
 
     def ids_of(g, hub=False):
         if hub:
@@ -351,27 +361,20 @@
         data_wait(g, (2 * g + lo) * tables, tables)
         total_ref[...] += data_recv[slot_of(2 * g + lo)]
 
-    def add_mixed(g):
-        late = tables // 2
-        data_wait(g, 2 * g * tables, tables + late)
-        total_ref[...] += data_recv[slot_of(2 * g + lo)]
-        total_ref[late:] += data_recv[pl.ds((2 * g + 1 - lo) * tables + late, late)]
-
     def planned(r):
-        sends = {DIRECT: direct, PAIR: paired, MIXED: mixed}
-        adds = {DIRECT: add_direct, PAIR: add_paired, MIXED: add_mixed}
-        plan = PLANS[far][r]
-        for op, g in plan:
+        sends = {DIRECT: direct, PAIR: paired}
+        adds = {DIRECT: add_direct, PAIR: add_paired}
+        for op, g in PLANS[far][r]:
             if op == OWN:
                 own_group(r)
             elif op == FORWARD:
-                forward(g, chunks // 2 if (MIXED, g) in plan else chunks)
+                forward(g)
             else:
                 ids_of(g, r == 1 and g == 0)
                 compute(g, sends[op])
         add_own(r)
         for g in ARRIVALS[far][r]:
-            adds[next(op for op, to in PLANS[far][g] if op in adds and to == r)](g)
+            adds[DIRECT if (DIRECT, r) in PLANS[far][g] else PAIR](g)
 
     def others(action):
         def both(m):
@@ -399,7 +402,7 @@
             compute(g, paired)
 
         others(far_group)
-        others(lambda g: forward(g, chunks))
+        others(forward)
         add_own(hi)
         add_direct(near)
         others(add_paired)
@@ -432,6 +435,11 @@
             device_id={"cols": at},
             device_id_type=MESH,
         )
+
+
+    @pl.when(col < cols - 1)
+    def _():
+        pl.semaphore_wait(ready_sem, cols - 1 - col)
 
     for j in range(1, cols):
         gram_copy(col, (col + j) % cols).start()
@@ -519,7 +527,7 @@
     chunks = CHUNKS
     any_space = pl.BlockSpec(memory_space=pl.ANY)
     pair_rows = -(-pairs // 8) * 8
-    tile = (2 * count, 2 * cap)
+    tile = (count, 2 * cap)
     pooled, inter = pl.pallas_call(
         functools.partial(kernel, n, cols, fan),
         out_shape=(
@@ -552,6 +560,7 @@
             pltpu.SemaphoreType.DMA((far,)),
             pltpu.SemaphoreType.DMA((1,)),
             pltpu.SemaphoreType.DMA((1,)),
+            pltpu.SemaphoreType.REGULAR,
         ],
         compiler_params=pltpu.CompilerParams(collective_id=0, has_side_effects=True),
     )(tables, dense_features, slot_rows, slot_examples, slot_counts.transpose(0, 2, 1))

time: 21.3 us -> 21.4 us (level)
  no operation moved by 1% of the time
where the time goes in v4:
time: 21.4 us; the launch traced here: 21.2 us
  Pallas kernels  20.6 us (96%)
  between operations  0.64 us (3%)
    pallas_call x1, Pallas kernels, body(): pl.pallas_call(functools.partial(kernel, n, cols, fan), out_shape=(pltpu....  19.9 us
    pallas_call x1, Pallas kernels, write_out(): pl.pallas_call(store, out_shape=(jax.ShapeDtypeStruct(pooled.shape, poole...  0.65 us

profile of v4, /device:TPU:0, one launch (start us, length us, event | category | flops | bytes accessed | tf_op | source)
XLA Modules:
  0.0 21.2 jit_solution(8484695643285609028)
XLA Ops:
  0.6 19.9 %shard_map.68 = (f32[32,4,128]{2,1,0:T(4,128)S(1)}, f32[10,32]{1,0:T(8,128)S(1)}) custom-call(f32[4,512,128]{2,1,0:T(8,128)} %tables_hbm.1, f32[32,128]{1,0:T(8,128)} %dense_hbm.1, s32[1,8,4,64]{3,2,1,0:T(4,128)} %rows_hbm.1, s32[1,8,4,64]{3,2,1,0:T(4,128)} %examples_hbm.1, s32[1,4,8]{2,1,0:T(4,128)} %bitcast.2), custom_call_target="tpu_custom_call" | custom-call | tf_op jit(solution)/shard_map/pallas_call | solution.py:531
  20.6 0.7 %shard_map.69 = (f32[32,4,128]{2,1,0:T(4,128)}, f32[10,32]{1,0:T(8,128)}) custom-call(f32[32,4,128]{2,1,0:T(4,128)S(1)} %get-tuple-element.6.pooled_ref, f32[10,32]{1,0:T(8,128)S(1)} %get-tuple-element.7.inter_ref), custom_call_target="tpu_custom_call" | custom-call | tf_op jit(solution)/shard_map/pallas_call | solution.py:505

commit v5 on v4

--- a/solution.py
+++ b/solution.py
@@ -284,7 +284,7 @@
             src_ref=cross.at[g, piece],
             dst_ref=pair_recv.at[g, piece],
             send_sem=data_ssem.at[0],
-            recv_sem=pair_rsem.at[(g - hi - 1) % far, c],
+            recv_sem=pair_rsem.at[g % pair_rsem.shape[0], c],
             device_id={"rows": mate},
             device_id_type=MESH,
         )
@@ -555,7 +555,7 @@
             pltpu.SemaphoreType.DMA((1,)),
             pltpu.SemaphoreType.DMA((far,)),
             pltpu.SemaphoreType.DMA((1,)),
-            pltpu.SemaphoreType.DMA((far - 1, chunks)),
+            pltpu.SemaphoreType.DMA((2 if far in PLANS else far, chunks)),
             pltpu.SemaphoreType.DMA((1,)),
             pltpu.SemaphoreType.DMA((far,)),
             pltpu.SemaphoreType.DMA((1,)),

time: 21.4 us -> 21.3 us (level)
  no operation moved by 1% of the time
where the time goes in v5:
time: 21.3 us; the launch traced here: 21.2 us
  Pallas kernels  20.5 us (96%)
  between operations  0.64 us (3%)
    pallas_call x1, Pallas kernels, body(): pl.pallas_call(functools.partial(kernel, n, cols, fan), out_shape=(pltpu....  19.9 us
    pallas_call x1, Pallas kernels, write_out(): pl.pallas_call(store, out_shape=(jax.ShapeDtypeStruct(pooled.shape, poole...  0.65 us

profile of v5, /device:TPU:0, one launch (start us, length us, event | category | flops | bytes accessed | tf_op | source)
XLA Modules:
  0.0 21.2 jit_solution(8575090553389498608)
XLA Ops:
  0.6 19.9 %shard_map.68 = (f32[32,4,128]{2,1,0:T(4,128)S(1)}, f32[10,32]{1,0:T(8,128)S(1)}) custom-call(f32[4,512,128]{2,1,0:T(8,128)} %tables_hbm.1, f32[32,128]{1,0:T(8,128)} %dense_hbm.1, s32[1,8,4,64]{3,2,1,0:T(4,128)} %rows_hbm.1, s32[1,8,4,64]{3,2,1,0:T(4,128)} %examples_hbm.1, s32[1,4,8]{2,1,0:T(4,128)} %bitcast.2), custom_call_target="tpu_custom_call" | custom-call | tf_op jit(solution)/shard_map/pallas_call | solution.py:531
  20.5 0.7 %shard_map.69 = (f32[32,4,128]{2,1,0:T(4,128)}, f32[10,32]{1,0:T(8,128)}) custom-call(f32[32,4,128]{2,1,0:T(4,128)S(1)} %get-tuple-element.6.pooled_ref, f32[10,32]{1,0:T(8,128)S(1)} %get-tuple-element.7.inter_ref), custom_call_target="tpu_custom_call" | custom-call | tf_op jit(solution)/shard_map/pallas_call | solution.py:505
